TPU v7x, 32 devices: a whole 2x2x4 slice. The times are simulated.
32 devices in a mesh: pool: 2 (over x), seq: 4 (over y, core), head: 4 (over z).
Axes of the slice: x: 2, y: 2, z: 4, core: 2. Of those that a mesh axis runs over, the one named last changes fastest.
Arguments:
- prompt: bfloat16 [8, 2048, 8192], P('pool', 'seq'), may hold values from -6 to 6
- key_value_weight: bfloat16 [8192, 2, 1024], P('seq', None, 'head'), may hold values from -0.0625 to 0.0625
- adapter_down_weight: bfloat16 [8192, 256], P('seq'), may hold values from -0.0625 to 0.0625
- adapter_up_weight: bfloat16 [8, 2, 16, 1024], P(None, None, None, 'head'), may hold values from -0.75 to 0.75
- request_adapter_index: int32 [8], P('pool'), may hold values from 0 to 7
- destination: int32 [8], replicated, may hold values from 0 to 3, as said below
- rotated_query: bfloat16 [384, 8192], P(('pool', 'seq'), 'head'), may hold values from -150 to 150
- key_value_cache: bfloat16 [384, 128, 2, 1024], P(('pool', 'seq'), None, None, 'head'), may hold values from -6 to 6
- current_key_value: bfloat16 [384, 2, 1024], P(('pool', 'seq'), None, 'head'), may hold values from -6 to 6
- cached_length: int32 [384], P(('pool', 'seq')), may hold values from 1 to 128
- row_adapter_index: int32 [384], P('pool'), may hold values from 0 to 7
- output_weight: bfloat16 [8192, 8192], P('head', 'seq'), may hold values from -0.0625 to 0.0625
- output_down_weight: bfloat16 [8192, 8, 16], P('head'), may hold values from -0.0625 to 0.0625
- output_up_weight: bfloat16 [8, 16, 8192], P(None, None, 'seq'), may hold values from -3.59375 to 3.59375
Outputs:
- handed: bfloat16 [8, 2, 2048, 2, 1024], P(('pool', 'seq'), None, None, None, 'head')
- decoded: bfloat16 [384, 8192], P(('pool', 'head'), 'seq')
Inputs may be any that keep to these rules, and one draw needn't show every extreme that they name: `destination`: among one pool's 4 requests no decode owner is named more than 2 times, and some owner exactly 2 times; in each pool owners 0 and 3 both receive requests.
All inputs are finite; a program needn't handle non-finite values.
Results may differ from a plain program's by a relative error of at most 0.0085.
Values may be sent and summed in bfloat16 or wider, within the bound.
A program may use at most 128 MiB of HBM per device.

v0:
```python
import jax
import jax.numpy as jnp
from jax import lax
from jax.sharding import PartitionSpec as P

HEAD_DIM = 128
ADAPTER_RANK = 16
ADAPTER_COUNT = 8
CAP = 2


def swapped(value, axis, distance):
    mask = 2**distance
    pairs = [(source, source ^ mask) for source in range(lax.axis_size(axis))]
    return lax.ppermute(value, axis, pairs)


def attend_local(query_matrix, key_value_cache, prefill_state, lengths):
    decode_count = query_matrix.shape[0]
    kv_heads = key_value_cache.shape[-1] // HEAD_DIM
    query_groups = query_matrix.shape[1] // HEAD_DIM // kv_heads
    positions = key_value_cache.shape[1]
    query_batch = query_matrix.reshape(decode_count, kv_heads, query_groups, HEAD_DIM)
    key_matrix = key_value_cache[:, :, 0].reshape(decode_count, positions, kv_heads, HEAD_DIM)
    value_matrix = key_value_cache[:, :, 1].reshape(decode_count, positions, kv_heads, HEAD_DIM)
    prefill_key = prefill_state[:, 0].reshape(decode_count, kv_heads, HEAD_DIM)
    prefill_value = prefill_state[:, 1].reshape(decode_count, kv_heads, HEAD_DIM)
    factor = HEAD_DIM ** (-0.5)
    scores = (
        jnp.einsum("rkgd,rckd->rkgc", query_batch, key_matrix, preferred_element_type=jnp.float32)
        * factor
    )
    own_score = (
        jnp.einsum("rkgd,rkd->rkg", query_batch, prefill_key, preferred_element_type=jnp.float32)
        * factor
    )
    valid = (jnp.arange(positions, dtype=jnp.int32)[None, :] < lengths[:, None])[:, None, None, :]
    highest = jnp.maximum(jnp.max(jnp.where(valid, scores, -1e30), axis=-1), own_score)
    raw = jnp.where(valid, jnp.exp(scores - highest[..., None]), 0.0)
    own_raw = jnp.exp(own_score - highest)
    normer = jnp.sum(raw, axis=-1) + own_raw
    weights = (raw / normer[..., None]).astype(jnp.bfloat16)
    own_weight = (own_raw / normer).astype(jnp.bfloat16)
    mixed = jnp.einsum("rkgc,rckd->rkgd", weights, value_matrix, preferred_element_type=jnp.float32)
    mixed = (
        mixed
        + own_weight.astype(jnp.float32)[..., None]
        * prefill_value.astype(jnp.float32)[:, :, None, :]
    )
    return mixed.reshape(decode_count, kv_heads * query_groups * HEAD_DIM).astype(jnp.bfloat16)


def place_slots(owner_ids, block, decoders):
    requests = block.shape[0]
    order_index = jnp.arange(requests, dtype=jnp.int32)
    same_owner = owner_ids[:, None] == owner_ids[None, :]
    slot_of = jnp.sum(
        (same_owner & (order_index[None, :] < order_index[:, None])).astype(jnp.int32), axis=1
    )
    slot_hit = slot_of[None, :] == jnp.arange(CAP, dtype=jnp.int32)[:, None]
    owner_hit = owner_ids[None, :] == jnp.arange(decoders, dtype=jnp.int32)[:, None]
    placer = (slot_hit[:, None, :] & owner_hit[None, :, :]).astype(jnp.bfloat16)
    flat = block.reshape(requests, block.shape[1] * block.shape[2] * block.shape[3])
    outgoing = jnp.einsum("cdr,rx->cdx", placer, flat, preferred_element_type=jnp.float32)
    return outgoing.astype(jnp.bfloat16).reshape(
        CAP, decoders, block.shape[1], block.shape[2], block.shape[3]
    )


def body(
    prompt,
    key_value_weight,
    adapter_down_weight,
    adapter_up_weight,
    request_adapter_index,
    destination,
    rotated_query,
    key_value_cache,
    current_key_value,
    cached_length,
    row_adapter_index,
    output_weight,
    output_down_weight,
    output_up_weight,
):
    requests, tok_dev, model_width = prompt.shape
    key_value_width = key_value_weight.shape[2]
    token_matrix = prompt.reshape(requests * tok_dev, model_width)
    weight_rows = lax.all_gather(key_value_weight, "seq", axis=0, tiled=True)
    lowered_rows = lax.all_gather(adapter_down_weight, "seq", axis=0, tiled=True)
    decode_count = weight_rows.shape[0]
    base_part = jnp.dot(
        token_matrix,
        weight_rows.reshape(decode_count, 2 * key_value_width),
        preferred_element_type=jnp.float32,
    )
    low_part = jnp.dot(token_matrix, lowered_rows, preferred_element_type=jnp.float32)
    reduced_everything = low_part
    adapter_selector = (
        request_adapter_index[:, None] == jnp.arange(ADAPTER_COUNT, dtype=jnp.int32)[None, :]
    )
    reduced_everything = reduced_everything.reshape(
        requests, tok_dev, ADAPTER_COUNT, 2, ADAPTER_RANK
    )
    low_rank = jnp.sum(
        jnp.where(adapter_selector[:, None, :, None, None], reduced_everything, 0.0), axis=2
    )
    selected_up_weight = jnp.einsum(
        "um,mdzt->udzt",
        adapter_selector.astype(jnp.bfloat16),
        adapter_up_weight,
        preferred_element_type=jnp.float32,
    )
    correction = jnp.einsum(
        "rtkq,rkqf->rtkf", low_rank, selected_up_weight, precision=lax.Precision.HIGHEST
    )
    prefilled = (base_part.reshape(requests, tok_dev, 2, key_value_width) + correction).astype(
        jnp.bfloat16
    )
    decoders = lax.axis_size("seq")
    pool_index = lax.axis_index("pool")
    other_owners = lax.dynamic_slice_in_dim(destination, (1 - pool_index) * requests, requests)
    arrived = swapped(prefilled, "pool", 0)
    outgoing = place_slots(other_owners, arrived, decoders)
    handed = lax.all_to_all(outgoing, "seq", split_axis=1, concat_axis=1, tiled=True)
    handed = handed.reshape(1, CAP, decoders * tok_dev, 2, key_value_width)
    attended = attend_local(rotated_query, key_value_cache, current_key_value, cached_length)
    down_flat = output_down_weight.reshape(
        output_down_weight.shape[0], ADAPTER_COUNT * ADAPTER_RANK
    )
    up_flat = output_up_weight.reshape(
        ADAPTER_COUNT * ADAPTER_RANK, output_up_weight.shape[2]
    ).astype(jnp.float32)
    rank_owner = jnp.arange(ADAPTER_COUNT * ADAPTER_RANK, dtype=jnp.int32) // ADAPTER_RANK
    attn_rows = lax.all_gather(attended, "seq", axis=0, tiled=True)
    low_rows = jnp.dot(attn_rows, down_flat, preferred_element_type=jnp.float32)
    low_rows = jnp.where(row_adapter_index[:, None] == rank_owner[None, :], low_rows, 0.0)
    projected = jnp.dot(attn_rows, output_weight, preferred_element_type=jnp.float32)
    terms = projected + jnp.dot(low_rows, up_flat, precision=lax.Precision.HIGHEST)
    decoded = lax.psum_scatter(terms, "head", scatter_dimension=0, tiled=True)
    return (handed, decoded.astype(jnp.bfloat16))


def solution(mesh):
    in_specs = (
        P("pool", "seq", None),
        P("seq", None, "head"),
        P("seq", None),
        P(None, None, None, "head"),
        P("pool"),
        P(),
        P(("pool", "seq"), "head"),
        P(("pool", "seq"), None, None, "head"),
        P(("pool", "seq"), None, "head"),
        P(("pool", "seq")),
        P("pool"),
        P("head", "seq"),
        P("head", None, None),
        P(None, None, "seq"),
    )
    out_specs = (P(("pool", "seq"), None, None, None, "head"), P(("pool", "head"), "seq"))
    return jax.shard_map(body, mesh=mesh, in_specs=in_specs, out_specs=out_specs, check_vma=False)
```

profile of v0, /device:TPU:0, one launch (start us, length us, event | category | flops | bytes accessed | tf_op | source)
XLA Modules:
  0.0 321.1 jit_solution(5121571751977776219)
XLA Ops:
  8.1 2.4 copy.68
  10.5 0.7 all-gather.3.cloned.1.call-update
  11.2 13.9 %fusion.29 = (bf16[48,128,1,256]{3,2,1,0:T(2,128)(2,1)}, bf16[48,128,1,256]{3,2,1,0:T(2,128)(2,1)}) fusion(bf16[48,128,2,256]{3,2,1,0:T(2,128)(2,1)} %param.21), kind=kLoop, calls=%fused_computation.52 | loop fusion | bytes 12582912 | tf_op jit(solution)/shard_map/slice | solution.py:24
  25.2 13.5 %copy.93 = bf16[48,128,1,256]{1,3,0,2:T(8,128)(2,1)} copy(bf16[48,128,1,256]{3,2,1,0:T(2,128)(2,1)} %get-tuple-element.8) | data formatting | bytes 6291456
  38.8 2.9 select_reduce_fusion.1
  41.8 0.2 fusion.17
  42.3 0.4 fusion.9
  42.9 13.6 %copy.94 = bf16[48,128,1,256]{1,3,0,2:T(8,128)(2,1)} copy(bf16[48,128,1,256]{3,2,1,0:T(2,128)(2,1)} %get-tuple-element.9) | data formatting | bytes 6291456
  56.7 0.2 fusion.15
  56.9 4.2 %fusion.8 = bf16[48,2,8,128]{3,2,1,0:T(8,128)(2,1)S(1)} fusion(bf16[48,128,2,128]{1,3,2,0:T(8,128)(2,1)} %bitcast.84, f32[48,2,8,128]{3,2,1,0:T(8,128)S(1)} %get-tuple-element.13, f32[48,2,128]{2,1,0:T(2,128)S(1)} %bitcast.91, f32[48,2,8]{2,1,0:T(2,128)S(1)} %copy.82, f32[48,2,8]{2,1,0:T(2,128)S(1)} %copy.79, f32[48,2,8]{2,1,0:T(2,128)S(1)} %copy.77, ...), kind=kOutput, calls=%fused_computation.12 | convolution fusion | flops 25853952 | bytes 3800064 | tf_op jit(solution)/shard_map/rkgc,rckd->rkgd/dot_general | solution.py:44
  61.1 16.6 %select_reduce_fusion = f32[4,512,2,16]{1,3,2,0:T(8,128)S(1)} fusion(bf16[8,2,16,8192,1]{3,2,1,0,4:T(8,128)(2,1)} %bitcast.92, bf16[4,512,8192]{2,1,0:T(8,128)(2,1)} %param.14, pred[4,8]{1,0:T(4,128)(4,1)S(1)} %iota_compare_fusion.1), kind=kOutput, calls=%fused_computation.9 | convolution fusion | flops 8590917632 | bytes 38010912 | tf_op jit(solution)/shard_map/dot_general | solution.py:97
  77.7 29.9 %all-gather.3.cloned.1.call-done = bf16[8192,2,256]{2,1,0:T(2,128)(2,1)} async-done(((bf16[2048,2,256]{2,1,0:T(2,128)(2,1)}), bf16[8192,2,256]{2,1,0:T(2,128)(2,1)}) %all-gather.3.cloned.1.call-update) | async-done | bytes 8388624 | tf_op jit(solution)/shard_map/all_gather | solution.py:89
  107.6 21.2 %copy.92 = bf16[8192,2,256]{0,2,1:T(8,128)(2,1)} copy(bf16[8192,2,256]{2,1,0:T(2,128)(2,1)} %all-gather.3.cloned.1.call-done) | data formatting | bytes 16777216 | tf_op jit(solution)/shard_map/reshape | solution.py:94
  128.8 23.9 %fusion.2 = f32[4,512,2,256]{3,1,2,0:T(8,128)S(1)} fusion(bf16[4,512,8192]{2,1,0:T(8,128)(2,1)} %param.14, bf16[8192,2,256]{0,2,1:T(8,128)(2,1)} %copy.92), kind=kOutput, calls=%fused_computation.3 | convolution fusion | flops 17179869184 | bytes 46137344 | tf_op jit(solution)/shard_map/dot_general | solution.py:92
  152.7 4.0 %fusion.5 = bf16[4,512,2,256]{3,1,2,0:T(8,128)(2,1)S(1)} fusion(f32[4,512,2,256]{3,1,2,0:T(8,128)S(1)} %fusion.2, f32[4,512,2,16]{1,3,2,0:T(8,128)S(1)} %select_reduce_fusion, f32[4,2,16,256]{3,0,2,1:T(4,128)S(1)} %fusion.15), kind=kOutput, calls=%fused_computation.7 | convolution fusion | flops 203423744 | bytes 6684672 | tf_op jit(solution)/shard_map/rtkq,rkqf->rtkf/dot_general | solution.py:114
  156.7 1.5 collective-permute-start
  158.3 8.6 %all_gather.11 = bf16[192,2048]{1,0:T(8,128)(2,1)S(1)} all-gather(bf16[48,2048]{1,0:T(8,128)(2,1)S(1)} %bitcast.87), channel_id=1, replica_groups=mesh['pool'=2,'seq'=4,'head'=4] {'seq'}, dimensions={0}, use_global_device_ids=true | all-gather | bytes 983040 | tf_op jit(solution)/shard_map/all_gather | solution.py:135
  166.8 0.4 convolution_select_fusion
  167.2 5.2 %fusion.30 = f32[192,2048]{1,0:T(8,128)S(1)} fusion(bf16[192,2048]{1,0:T(8,128)(2,1)S(1)} %all_gather.11, bf16[2048,2048]{1,0:T(8,128)(2,1)} %param.25), kind=kOutput, calls=%fused_computation.53 | convolution fusion | flops 1610612736 | bytes 10747904 | tf_op jit(solution)/shard_map/dot_general | solution.py:138
  172.4 2.0 convolution_add_fusion
  174.5 0.2 convert_reduce_fusion
  174.7 29.9 %collective-permute-done = bf16[4,512,2,256]{3,1,2,0:T(8,128)(2,1)} collective-permute-done((bf16[4,512,2,256]{3,1,2,0:T(8,128)(2,1)S(1)}, bf16[4,512,2,256]{3,1,2,0:T(8,128)(2,1)}, u32[]{:S(2)}, u32[]{:S(2)}) %collective-permute-start) | collective-permute-done | bytes 2097184 | tf_op jit(solution)/shard_map/ppermute | solution.py:15
  204.6 5.1 %copy.71 = bf16[4,512,2,256]{3,2,1,0:T(2,128)(2,1)} copy(bf16[4,512,2,256]{3,1,2,0:T(8,128)(2,1)} %collective-permute-done) | data formatting | bytes 4194304 | tf_op jit(solution)/shard_map/ppermute | solution.py:15
  209.7 2.9 reshape.147
  212.6 3.7 %convolution_convert_fusion = bf16[2,4,262144]{2,1,0:T(4,128)(2,1)} fusion(bf16[4,262144,1]{1,0,2:T(4,128)(2,1)S(1)} %reshape.147, pred[4,4]{1,0:T(4,128)(4,1)S(1)} %iota_compare_fusion.2, pred[2,4]{1,0:T(4,128)(4,1)S(1)} %iota_compare_fusion.4), kind=kOutput, calls=%fused_computation | convolution fusion | flops 18874400 | bytes 6291480 | tf_op jit(solution)/shard_map/cdr,rx->cdx/dot_general | solution.py:64
  216.3 7.1 %reshape.136 = bf16[2,4,512,2,256]{4,3,2,1,0:T(2,128)(2,1)} reshape(bf16[2,4,262144]{2,1,0:T(4,128)(2,1)} %convolution_convert_fusion) | data formatting | bytes 8388608 | tf_op jit(solution)/shard_map/reshape | solution.py:65
  223.4 7.1 %copy.72 = bf16[2,4,512,2,256]{4,3,2,0,1:T(2,128)(2,1)} copy(bf16[2,4,512,2,256]{4,3,2,1,0:T(2,128)(2,1)} %reshape.136) | data formatting | bytes 8388608 | tf_op jit(solution)/shard_map/reshape | solution.py:65
  230.5 4.8 %all-to-all-start = ((bf16[2,4,512,2,256]{4,3,2,0,1:T(2,128)(2,1)}), bf16[2,4,512,2,256]{4,3,2,0,1:T(2,128)(2,1)}, u32[]{:S(2)}, u32[]{:S(2)}) async-start(bf16[2,4,512,2,256]{4,3,2,0,1:T(2,128)(2,1)} %copy.72), calls=%async_computation | async-start | bytes 8388608 | tf_op jit(solution)/shard_map/all_to_all | solution.py:125
  235.4 1.7 convert_element_type.50
  237.1 46.5 %all-to-all-done = bf16[2,4,512,2,256]{4,3,2,0,1:T(2,128)(2,1)} async-done(((bf16[2,4,512,2,256]{4,3,2,0,1:T(2,128)(2,1)}), bf16[2,4,512,2,256]{4,3,2,0,1:T(2,128)(2,1)}, u32[]{:S(2)}, u32[]{:S(2)}) %all-to-all-start) | async-done | bytes 4194336 | tf_op jit(solution)/shard_map/all_to_all | solution.py:125
  283.6 2.9 copy.73
  286.4 27.2 %copy.83 = bf16[1,2,2048,2,256]{4,3,2,1,0:T(2,128)(2,1)} copy(bf16[1,2,2048,2,256]{4,2,3,1,0:T(8,128)(2,1)S(1)} %bitcast.82) | data formatting | bytes 8388608
  (42 shorter events, 1.1 us)
Async XLA Ops:
  8.0 164.4 %copy-start = (bf16[8,16,2048]{2,1,0:T(8,128)(2,1)S(1)}, bf16[8,16,2048]{2,1,0:T(8,128)(2,1)}, u32[]{:S(2)}) copy-start(bf16[8,16,2048]{2,1,0:T(8,128)(2,1)} %param.27) | copy-start | bytes 1572868
  8.0 53.1 %all-gather.5.cloned.1.call-start = ((), (), s32[]{:S(2)}) async-start(), calls=%async_computation.3 | async-start | bytes 5242880 | tf_op jit(solution)/shard_map/all_gather | solution.py:90
  10.4 97.2 %all-gather.3.cloned.1.call-start = ((), (), s32[]{:S(2)}) async-start(), calls=%async_computation.2 | async-start | bytes 10485760 | tf_op jit(solution)/shard_map/all_gather | solution.py:89
  11.2 224.2 %reduce-scatter.2.cloned.1.call-start = ((), (), s32[]{:S(2)}) async-start(), calls=%async_computation.4 | async-start | bytes 1966080 | tf_op jit(solution)/shard_map/reduce_scatter | solution.py:140
  25.1 13.6 %copy-start.2 = (bf16[48,2048]{1,0:T(8,128)(2,1)S(1)}, bf16[48,2048]{1,0:T(8,128)(2,1)}, u32[]{:S(2)}) copy-start(bf16[48,2048]{1,0:T(8,128)(2,1)} %param.20) | copy-start | bytes 589828
  25.1 13.6 %copy-start.7 = (s32[48]{0:T(128)S(1)}, s32[48]{0:T(128)}, u32[]{:S(2)}) copy-start(s32[48]{0:T(128)} %param.23) | copy-start | bytes 580
  38.7 3.1 copy-start.4
  42.9 13.6 %copy-start.6 = (s32[4]{0:T(128)S(1)}, s32[4]{0:T(128)}, u32[]{:S(2)}) copy-start(s32[4]{0:T(128)} %param.18) | copy-start | bytes 52
  42.9 13.7 %copy-start.3 = (bf16[8,2,16,256]{3,2,1,0:T(8,128)(2,1)S(1)}, bf16[8,2,16,256]{3,2,1,0:T(8,128)(2,1)}, u32[]{:S(2)}) copy-start(bf16[8,2,16,256]{3,2,1,0:T(8,128)(2,1)} %param.17) | copy-start | bytes 393220
  152.7 14.1 %copy-start.1 = (bf16[2048,8,16]{0,2,1:T(8,128)(2,1)S(1)}, bf16[2048,8,16]{0,2,1:T(8,128)(2,1)}, u32[]{:S(2)}) copy-start(bf16[2048,8,16]{0,2,1:T(8,128)(2,1)} %param.26) | copy-start | bytes 1572868
  152.7 14.1 %copy-start.5 = (s32[192]{0:T(256)S(1)}, s32[192]{0:T(256)}, u32[]{:S(2)}) copy-start(s32[192]{0:T(256)} %param.24) | copy-start | bytes 2308
  156.7 47.9 %collective-permute-start = (bf16[4,512,2,256]{3,1,2,0:T(8,128)(2,1)S(1)}, bf16[4,512,2,256]{3,1,2,0:T(8,128)(2,1)}, u32[]{:S(2)}, u32[]{:S(2)}) collective-permute-start(bf16[4,512,2,256]{3,1,2,0:T(8,128)(2,1)S(1)} %fusion.5), channel_id=1, source_target_pairs={{0,16},{16,0},{1,17},{17,1},{2,18},{18,2},{3,19},{19,3},{4,20},{20... | collective-permute-start | bytes 6291464 | tf_op jit(solution)/shard_map/ppermute | solution.py:15
  172.4 2.0 copy-start.8
  230.5 53.0 %all-to-all-start = ((bf16[2,4,512,2,256]{4,3,2,0,1:T(2,128)(2,1)}), bf16[2,4,512,2,256]{4,3,2,0,1:T(2,128)(2,1)}, u32[]{:S(2)}, u32[]{:S(2)}) async-start(bf16[2,4,512,2,256]{4,3,2,0,1:T(2,128)(2,1)} %copy.72), calls=%async_computation | async-start | bytes 8388608 | tf_op jit(solution)/shard_map/all_to_all | solution.py:125
Sparse Core Ops, SparseCore 0:
  10.6 37.1 all-gather.4
  49.3 58.2 all-gather.2
Sparse Core Ops, SparseCore 1:
  174.5 34.7 reduce-scatter.1
where the time goes:
time: 323 us; the launch traced here: 321 us
  local copies, waits for them, and re-layouts  118 us (37%)
  waiting for transfers between devices  107 us (33%)
  matrix products  63.3 us (20%)
  between operations  15.7 us (5%)
  blocking collectives  8.55 us (3%)
  starting transfers between devices  6.5 us (2%)
    unnamed x24, local copies, waits for them, and re-layouts  56.8 us
    all_to_all x1, waiting for transfers between devices, body(): lax.all_to_all(outgoing, 'seq', split_axis=1, concat_axis=1, tiled=True)  46.5 us
    all_gather x1, waiting for transfers between devices, body(): weight_rows = lax.all_gather(key_value_weight, 'seq', axis=0, tiled=True)  29.9 us
    ppermute x1, waiting for transfers between devices, swapped(): return lax.ppermute(value, axis, pairs)  29.9 us
    dot_general x1, matrix products, body(): jnp.dot(token_matrix, weight_rows.reshape(decode_count, 2 * key_value_wid...  23.9 us
    reshape x1, local copies, waits for them, and re-layouts, body(): weight_rows.reshape(decode_count, 2 * key_value_width)  21.2 us
    dot_general x1, matrix products, body(): jnp.dot(token_matrix, lowered_rows, preferred_element_type=jnp.float32)  16.6 us
    reshape x2, local copies, waits for them, and re-layouts, place_slots(): outgoing.astype(jnp.bfloat16)  14.2 us
  transfers between devices with their start and end apart: 5, of which 3 were waited for; matrix products, arithmetic and copies ran while one was open for 32% of the time, Pallas kernels for 0%

commit v1 on v0

--- a/solution.py
+++ b/solution.py
@@ -122,7 +122,10 @@
     other_owners = lax.dynamic_slice_in_dim(destination, (1 - pool_index) * requests, requests)
     arrived = swapped(prefilled, "pool", 0)
     outgoing = place_slots(other_owners, arrived, decoders)
-    handed = lax.all_to_all(outgoing, "seq", split_axis=1, concat_axis=1, tiled=True)
+    handed = jnp.concatenate(
+        lax.all_to_all(jnp.stack(jnp.split(outgoing, lax.axis_size("seq"), axis=1)), "seq", 0, 0),
+        axis=1,
+    )
     handed = handed.reshape(1, CAP, decoders * tok_dev, 2, key_value_width)
     attended = attend_local(rotated_query, key_value_cache, current_key_value, cached_length)
     down_flat = output_down_weight.reshape(

time: 323 us -> 306 us (0.947)
  local copies, waits for them, and re-layouts: 118 us -> 91.9 us
  other arithmetic: 2.48 us -> 11 us
    unnamed x24 -> x23, local copies, waits for them, and re-layouts: 56.8 us -> 29.6 us
    another operation x0 -> x1, other arithmetic: none -> 8.55 us  [body(): jnp.stack(jnp.split(outgoing, lax.axis_size('seq'), axis=1))]
    reshape x0 -> x1, local copies, waits for them, and re-layouts: none -> 7.08 us  [body(): jnp.concatenate(lax.all_to_all(jnp.stack(jnp.split(outgoing, lax.axis_siz...]
    reshape x2 -> x1, local copies, waits for them, and re-layouts: 14.2 us -> 7.12 us  [place_slots(): outgoing.astype(jnp.bfloat16)]
    another operation x0 -> x1, local copies, waits for them, and re-layouts: none -> 4.43 us  [body(): jnp.stack(jnp.split(outgoing, lax.axis_size('seq'), axis=1))]
  transfers between devices with their start and end apart: 5 -> 5, of which waited for: 3 -> 3; matrix products, arithmetic and copies ran while one was open for 32% -> 35% of each run, Pallas kernels for 0% -> 0%
where the time goes in v1:
time: 306 us; the launch traced here: 304 us
  waiting for transfers between devices  107 us (35%)
  local copies, waits for them, and re-layouts  91.9 us (30%)
  matrix products  63.2 us (21%)
  between operations  15.7 us (5%)
  other arithmetic  11 us (4%)
  blocking collectives  8.55 us (3%)
  starting transfers between devices  6.51 us (2%)
    all_to_all x1, waiting for transfers between devices, body(): lax.all_to_all(jnp.stack(jnp.split(outgoing, lax.axis_size('seq'), axis=1...  46.5 us
    ppermute x1, waiting for transfers between devices, swapped(): return lax.ppermute(value, axis, pairs)  29.9 us
    all_gather x1, waiting for transfers between devices, body(): weight_rows = lax.all_gather(key_value_weight, 'seq', axis=0, tiled=True)  29.9 us
    unnamed x23, local copies, waits for them, and re-layouts  29.6 us
    dot_general x1, matrix products, body(): jnp.dot(token_matrix, weight_rows.reshape(decode_count, 2 * key_value_wid...  23.9 us
    reshape x1, local copies, waits for them, and re-layouts, body(): weight_rows.reshape(decode_count, 2 * key_value_width)  21.2 us
    dot_general x1, matrix products, body(): jnp.dot(token_matrix, lowered_rows, preferred_element_type=jnp.float32)  16.6 us
    slice x1, local copies, waits for them, and re-layouts, attend_local(): key_value_cache[:, :, 0]  13.9 us
  transfers between devices with their start and end apart: 5, of which 3 were waited for; matrix products, arithmetic and copies ran while one was open for 35% of the time, Pallas kernels for 0%

profile of v1, /device:TPU:0, one launch (start us, length us, event | category | flops | bytes accessed | tf_op | source)
XLA Modules:
  0.0 304.1 jit_solution(4150813999843720291)
XLA Ops:
  8.1 2.4 copy.67
  10.5 0.7 all-gather.3.cloned.1.call-update
  11.3 13.9 %fusion.29 = (bf16[48,128,1,256]{3,2,1,0:T(2,128)(2,1)}, bf16[48,128,1,256]{3,2,1,0:T(2,128)(2,1)}) fusion(bf16[48,128,2,256]{3,2,1,0:T(2,128)(2,1)} %param.21), kind=kLoop, calls=%fused_computation.57 | loop fusion | bytes 12582912 | tf_op jit(solution)/shard_map/slice | solution.py:24
  25.2 13.5 %copy.96 = bf16[48,128,1,256]{1,3,0,2:T(8,128)(2,1)} copy(bf16[48,128,1,256]{3,2,1,0:T(2,128)(2,1)} %get-tuple-element.2) | data formatting | bytes 6291456
  38.8 2.9 select_reduce_fusion.1
  41.8 0.2 fusion.17
  42.3 0.4 fusion.9
  42.9 13.6 %copy.97 = bf16[48,128,1,256]{1,3,0,2:T(8,128)(2,1)} copy(bf16[48,128,1,256]{3,2,1,0:T(2,128)(2,1)} %get-tuple-element.3) | data formatting | bytes 6291456
  56.7 0.2 fusion.15
  56.9 4.2 %fusion.8 = bf16[48,2,8,128]{3,2,1,0:T(8,128)(2,1)S(1)} fusion(bf16[48,128,2,128]{1,3,2,0:T(8,128)(2,1)} %bitcast.99, f32[48,2,8,128]{3,2,1,0:T(8,128)S(1)} %get-tuple-element.11, f32[48,2,128]{2,1,0:T(2,128)S(1)} %bitcast.106, f32[48,2,8]{2,1,0:T(2,128)S(1)} %copy.83, f32[48,2,8]{2,1,0:T(2,128)S(1)} %copy.80, f32[48,2,8]{2,1,0:T(2,128)S(1)} %copy.78, ...), kind=kOutput, calls=%fused_computation.13 | convolution fusion | flops 25853952 | bytes 3800064 | tf_op jit(solution)/shard_map/rkgc,rckd->rkgd/dot_general | solution.py:44
  61.1 16.6 %select_reduce_fusion = f32[4,512,2,16]{1,3,2,0:T(8,128)S(1)} fusion(bf16[8,2,16,8192,1]{3,2,1,0,4:T(8,128)(2,1)} %bitcast.107, bf16[4,512,8192]{2,1,0:T(8,128)(2,1)} %param.14, pred[4,8]{1,0:T(4,128)(4,1)S(1)} %iota_compare_fusion.1), kind=kOutput, calls=%fused_computation.10 | convolution fusion | flops 8590917632 | bytes 38010912 | tf_op jit(solution)/shard_map/dot_general | solution.py:97
  77.7 29.9 %all-gather.3.cloned.1.call-done = bf16[8192,2,256]{2,1,0:T(2,128)(2,1)} async-done(((bf16[2048,2,256]{2,1,0:T(2,128)(2,1)}), bf16[8192,2,256]{2,1,0:T(2,128)(2,1)}) %all-gather.3.cloned.1.call-update) | async-done | bytes 8388624 | tf_op jit(solution)/shard_map/all_gather | solution.py:89
  107.6 21.2 %copy.92 = bf16[8192,2,256]{0,2,1:T(8,128)(2,1)} copy(bf16[8192,2,256]{2,1,0:T(2,128)(2,1)} %all-gather.3.cloned.1.call-done) | data formatting | bytes 16777216 | tf_op jit(solution)/shard_map/reshape | solution.py:94
  128.8 23.9 %fusion.2 = f32[4,512,2,256]{3,1,2,0:T(8,128)S(1)} fusion(bf16[4,512,8192]{2,1,0:T(8,128)(2,1)} %param.14, bf16[8192,2,256]{0,2,1:T(8,128)(2,1)} %copy.92), kind=kOutput, calls=%fused_computation.3 | convolution fusion | flops 17179869184 | bytes 46137344 | tf_op jit(solution)/shard_map/dot_general | solution.py:92
  152.8 3.9 %fusion.5 = bf16[4,512,2,256]{3,1,2,0:T(8,128)(2,1)S(1)} fusion(f32[4,512,2,256]{3,1,2,0:T(8,128)S(1)} %fusion.2, f32[4,512,2,16]{1,3,2,0:T(8,128)S(1)} %select_reduce_fusion, f32[4,2,16,256]{3,0,2,1:T(4,128)S(1)} %fusion.15), kind=kOutput, calls=%fused_computation.8 | convolution fusion | flops 203423744 | bytes 6684672 | tf_op jit(solution)/shard_map/rtkq,rkqf->rtkf/dot_general | solution.py:114
  156.7 1.5 collective-permute-start
  158.3 8.5 %all_gather.11 = bf16[192,2048]{1,0:T(8,128)(2,1)S(1)} all-gather(bf16[48,2048]{1,0:T(8,128)(2,1)S(1)} %bitcast.102), channel_id=1, replica_groups=mesh['pool'=2,'seq'=4,'head'=4] {'seq'}, dimensions={0}, use_global_device_ids=true | all-gather | bytes 983040 | tf_op jit(solution)/shard_map/all_gather | solution.py:138
  166.9 0.4 convolution_select_fusion
  167.2 5.2 %fusion.30 = f32[192,2048]{1,0:T(8,128)S(1)} fusion(bf16[192,2048]{1,0:T(8,128)(2,1)S(1)} %all_gather.11, bf16[2048,2048]{1,0:T(8,128)(2,1)} %param.25), kind=kOutput, calls=%fused_computation.58 | convolution fusion | flops 1610612736 | bytes 10747904 | tf_op jit(solution)/shard_map/dot_general | solution.py:141
  172.5 2.0 convolution_add_fusion
  174.5 0.2 convert_reduce_fusion
  174.8 29.9 %collective-permute-done = bf16[4,512,2,256]{3,1,2,0:T(8,128)(2,1)} collective-permute-done((bf16[4,512,2,256]{3,1,2,0:T(8,128)(2,1)S(1)}, bf16[4,512,2,256]{3,1,2,0:T(8,128)(2,1)}, u32[]{:S(2)}, u32[]{:S(2)}) %collective-permute-start) | collective-permute-done | bytes 2097184 | tf_op jit(solution)/shard_map/ppermute | solution.py:15
  204.7 5.1 %copy.70 = bf16[4,512,2,256]{3,2,1,0:T(2,128)(2,1)} copy(bf16[4,512,2,256]{3,1,2,0:T(8,128)(2,1)} %collective-permute-done) | data formatting | bytes 4194304 | tf_op jit(solution)/shard_map/ppermute | solution.py:15
  209.8 2.9 reshape.147
  212.7 3.7 %convolution_convert_fusion = bf16[2,4,262144]{2,1,0:T(4,128)(2,1)} fusion(bf16[4,262144,1]{1,0,2:T(4,128)(2,1)S(1)} %reshape.147, pred[4,4]{1,0:T(4,128)(4,1)S(1)} %iota_compare_fusion.2, pred[2,4]{1,0:T(4,128)(4,1)S(1)} %iota_compare_fusion.4), kind=kOutput, calls=%fused_computation | convolution fusion | flops 18874400 | bytes 6291480 | tf_op jit(solution)/shard_map/cdr,rx->cdx/dot_general | solution.py:64
  216.4 7.1 %reshape.136 = bf16[2,4,512,2,256]{4,3,2,1,0:T(2,128)(2,1)} reshape(bf16[2,4,262144]{2,1,0:T(4,128)(2,1)} %convolution_convert_fusion) | data formatting | bytes 8388608 | tf_op jit(solution)/shard_map/reshape | solution.py:65
  223.5 4.4 %slice_bitcast_fusion.3 = (bf16[1,2,1,512,2,256]{5,4,3,1,2,0:T(2,128)(2,1)S(1)}, bf16[1,2,1,512,2,256]{5,4,3,1,2,0:T(2,128)(2,1)S(1)}, bf16[1,2,1,512,2,256]{5,4...) fusion(bf16[2,4,512,2,256]{4,3,2,1,0:T(2,128)(2,1)} %reshape.136), kind=kLoop, calls=%fused_computation.18 | loop fusion | bytes 8388608 | tf_op jit(solution)/shard_map/stack | solution.py:126
  227.9 8.6 %pad_maximum_fusion = bf16[4,2,1,512,2,256]{5,4,3,1,2,0:T(2,128)(2,1)} fusion(bf16[1,2,1,512,2,256]{5,4,3,1,2,0:T(2,128)(2,1)S(1)} %get-tuple-element.6, bf16[1,2,1,512,2,256]{5,4,3,1,2,0:T(2,128)(2,1)S(1)} %get-tuple-element.7, bf16[1,2,1,512,2,256]{5,4,3,1,2,0:T(2,128)(2,1)S(1)} %get-tuple-element.5, bf16[1,2,1,512,2,256]{5,4,3,1,2,0:T(2,128)(2,1)S(1)} %get-tuple-element.4), kind=kLoop, calls=%fused_computation.6 | loop fusion | flops 6291456 | bytes 8388608 | tf_op jit(solution)/shard_map/stack | solution.py:126
  236.5 4.8 %all-to-all-start = ((bf16[4,2,1,512,2,256]{5,4,3,1,2,0:T(2,128)(2,1)}), bf16[4,2,1,512,2,256]{5,4,3,1,2,0:T(2,128)(2,1)}, u32[]{:S(2)}, u32[]{:S(2)}) async-start(bf16[4,2,1,512,2,256]{5,4,3,1,2,0:T(2,128)(2,1)} %pad_maximum_fusion), calls=%async_computation | async-start | bytes 8388608 | tf_op jit(solution)/shard_map/all_to_all | solution.py:126
  241.4 1.7 convert_element_type.50
  243.1 46.5 %all-to-all-done = bf16[4,2,1,512,2,256]{5,4,3,1,2,0:T(2,128)(2,1)} async-done(((bf16[4,2,1,512,2,256]{5,4,3,1,2,0:T(2,128)(2,1)}), bf16[4,2,1,512,2,256]{5,4,3,1,2,0:T(2,128)(2,1)}, u32[]{:S(2)}, u32[]{:S(2)}) %all-to-all-start) | async-done | bytes 4194336 | tf_op jit(solution)/shard_map/all_to_all | solution.py:126
  289.5 7.1 %copy.74 = bf16[2,4,1,512,2,256]{5,4,3,1,0,2:T(2,128)(2,1)} copy(bf16[2,4,1,512,2,256]{5,4,3,0,2,1:T(2,128)(2,1)} %bitcast.18) | data formatting | bytes 8388608 | tf_op jit(solution)/shard_map/reshape | solution.py:125
  (42 shorter events, 1.1 us)
Async XLA Ops:
  8.0 164.4 %copy-start = (bf16[8,16,2048]{2,1,0:T(8,128)(2,1)S(1)}, bf16[8,16,2048]{2,1,0:T(8,128)(2,1)}, u32[]{:S(2)}) copy-start(bf16[8,16,2048]{2,1,0:T(8,128)(2,1)} %param.27) | copy-start | bytes 1572868
  8.0 53.1 %all-gather.5.cloned.1.call-start = ((), (), s32[]{:S(2)}) async-start(), calls=%async_computation.3 | async-start | bytes 5242880 | tf_op jit(solution)/shard_map/all_gather | solution.py:90
  10.5 97.2 %all-gather.3.cloned.1.call-start = ((), (), s32[]{:S(2)}) async-start(), calls=%async_computation.2 | async-start | bytes 10485760 | tf_op jit(solution)/shard_map/all_gather | solution.py:89
  11.2 230.2 %reduce-scatter.2.cloned.1.call-start = ((), (), s32[]{:S(2)}) async-start(), calls=%async_computation.4 | async-start | bytes 1966080 | tf_op jit(solution)/shard_map/reduce_scatter | solution.py:143
  25.1 13.6 %copy-start.2 = (bf16[48,2048]{1,0:T(8,128)(2,1)S(1)}, bf16[48,2048]{1,0:T(8,128)(2,1)}, u32[]{:S(2)}) copy-start(bf16[48,2048]{1,0:T(8,128)(2,1)} %param.20) | copy-start | bytes 589828
  25.1 13.6 %copy-start.7 = (s32[48]{0:T(128)S(1)}, s32[48]{0:T(128)}, u32[]{:S(2)}) copy-start(s32[48]{0:T(128)} %param.23) | copy-start | bytes 580
  38.7 3.1 %copy-start.4 = (bf16[48,2,256]{2,1,0:T(2,128)(2,1)S(1)}, bf16[48,2,256]{2,1,0:T(2,128)(2,1)}, u32[]{:S(2)}) copy-start(bf16[48,2,256]{2,1,0:T(2,128)(2,1)} %param.22) | copy-start | bytes 147460
  42.9 13.6 %copy-start.6 = (s32[4]{0:T(128)S(1)}, s32[4]{0:T(128)}, u32[]{:S(2)}) copy-start(s32[4]{0:T(128)} %param.18) | copy-start | bytes 52
  42.9 13.7 %copy-start.3 = (bf16[8,2,16,256]{3,2,1,0:T(8,128)(2,1)S(1)}, bf16[8,2,16,256]{3,2,1,0:T(8,128)(2,1)}, u32[]{:S(2)}) copy-start(bf16[8,2,16,256]{3,2,1,0:T(8,128)(2,1)} %param.17) | copy-start | bytes 393220
  152.7 14.1 %copy-start.1 = (bf16[2048,8,16]{0,2,1:T(8,128)(2,1)S(1)}, bf16[2048,8,16]{0,2,1:T(8,128)(2,1)}, u32[]{:S(2)}) copy-start(bf16[2048,8,16]{0,2,1:T(8,128)(2,1)} %param.26) | copy-start | bytes 1572868
  152.8 14.1 %copy-start.5 = (s32[192]{0:T(256)S(1)}, s32[192]{0:T(256)}, u32[]{:S(2)}) copy-start(s32[192]{0:T(256)} %param.24) | copy-start | bytes 2308
  156.7 48.0 %collective-permute-start = (bf16[4,512,2,256]{3,1,2,0:T(8,128)(2,1)S(1)}, bf16[4,512,2,256]{3,1,2,0:T(8,128)(2,1)}, u32[]{:S(2)}, u32[]{:S(2)}) collective-permute-start(bf16[4,512,2,256]{3,1,2,0:T(8,128)(2,1)S(1)} %fusion.5), channel_id=1, source_target_pairs={{0,16},{16,0},{1,17},{17,1},{2,18},{18,2},{3,19},{19,3},{4,20},{20... | collective-permute-start | bytes 6291464 | tf_op jit(solution)/shard_map/ppermute | solution.py:15
  172.5 2.0 copy-start.8
  236.5 53.1 %all-to-all-start = ((bf16[4,2,1,512,2,256]{5,4,3,1,2,0:T(2,128)(2,1)}), bf16[4,2,1,512,2,256]{5,4,3,1,2,0:T(2,128)(2,1)}, u32[]{:S(2)}, u32[]{:S(2)}) async-start(bf16[4,2,1,512,2,256]{5,4,3,1,2,0:T(2,128)(2,1)} %pad_maximum_fusion), calls=%async_computation | async-start | bytes 8388608 | tf_op jit(solution)/shard_map/all_to_all | solution.py:126
Sparse Core Ops, SparseCore 0:
  10.6 37.1 all-gather.4
  49.3 58.2 all-gather.2
Sparse Core Ops, SparseCore 1:
  174.5 34.7 reduce-scatter.1
